TPU v7x, 32 devices: a whole 2x2x4 slice. The times are simulated.
32 devices in a mesh: section: 4 (over y, x), row: 8 (over z, core).
Axes of the slice: x: 2, y: 2, z: 4, core: 2. Of those that a mesh axis runs over, the one named last changes fastest.
Arguments:
- omega: bfloat16 [2048, 8192], P('section', 'row'), may hold values from -0.5 to 0.5
- basis: bfloat16 [8192, 1024], P('row', 'section'), may hold values from -6 to 6
- vectors: bfloat16 [4, 8192], P(None, 'row'), may hold values from -6 to 6
Outputs:
- ortho: float32 [4, 8192], P(None, ('row', 'section'))
- coeffs: float32 [4, 1024], P(None, 'section')
All inputs are finite; a program needn't handle non-finite values.
Results may differ from a plain program's by a relative error of at most 0.0021.
Values may be sent and summed in bfloat16 or wider, within the bound.
A program may use at most 64 MiB of HBM per device.

v0:
```python
import jax
import jax.numpy as jnp
from jax import lax
from jax.sharding import PartitionSpec as P


def from_behind(value, axis, steps):
    count = lax.axis_size(axis)
    initial, last = (max(0, -steps), min(count, count - steps))
    return lax.ppermute(value, axis, [(source, source + steps) for source in range(initial, last)])


def from_root(value, axis, source):
    kept = jnp.where(lax.axis_index(axis) == source, value, 0).astype(value.dtype)
    return lax.psum(kept, axis)


def lower_solve(factor, right):
    return lax.linalg.triangular_solve(factor, right, left_side=True, lower=True, transpose_a=False)


def factor_solve(factor, right):
    half = lower_solve(factor, right)
    return lax.linalg.triangular_solve(factor, half, left_side=True, lower=True, transpose_a=True)


def body(omega, basis, vectors):
    hi = lax.Precision.HIGHEST
    sections = lax.axis_size("section")
    my_section = lax.axis_index("section")
    whole = lax.all_gather(omega, "section", axis=0, tiled=True)
    sketch = lax.psum_scatter(
        jnp.dot(whole, basis, preferred_element_type=jnp.float32),
        "row",
        scatter_dimension=0,
        tiled=True,
    )
    probe_term = lax.dot_general(
        vectors, whole, (((1,), (1,)), ((), ())), preferred_element_type=jnp.float32
    )
    probe = lax.psum_scatter(probe_term, "row", scatter_dimension=1, tiled=True)
    gram = lax.psum(jnp.dot(sketch.T, sketch, precision=hi), "row")
    factor = jnp.linalg.cholesky(gram)

    def project(current):
        inner = jnp.dot(current, sketch, precision=hi)
        inner = lax.psum(inner, "row")
        coef = factor_solve(factor, inner.T).T
        return (coef, current - jnp.dot(coef, sketch.T, precision=hi))

    def advance(step, carry):
        current, kept = carry
        coef, moved = project(current)
        active = my_section == step
        kept = jnp.where(active, coef, kept)
        moved = jnp.where(active, moved, current)
        return (from_behind(moved, "section", 1), kept)

    start_coef = jnp.zeros((vectors.shape[0], basis.shape[1]), jnp.float32)
    probe, kept = lax.fori_loop(0, sections - 1, advance, (probe, start_coef))
    coef, moved = project(probe)
    finished = my_section == sections - 1
    kept = jnp.where(finished, coef, kept)
    final = from_root(moved, "section", sections - 1)
    rounded = kept.astype(jnp.bfloat16)
    own_term = lax.dot_general(
        rounded, basis, (((1,), (1,)), ((), ())), preferred_element_type=jnp.float32
    )
    removed = lax.psum_scatter(own_term, "section", scatter_dimension=1, tiled=True)
    width = removed.shape[1]
    mine = lax.dynamic_slice_in_dim(vectors, my_section * width, width, 1)
    remain = mine.astype(jnp.float32) - removed
    small = lax.psum(jnp.dot(final, final.T, precision=hi), "row")
    lower = jnp.linalg.cholesky(small)
    ortho = lower_solve(lower, remain)
    return (ortho, kept)


def solution(mesh):
    return jax.shard_map(
        body,
        mesh=mesh,
        in_specs=(P("section", "row"), P("row", "section"), P(None, "row")),
        out_specs=(P(None, ("row", "section")), P(None, "section")),
        check_vma=False,
    )
```

profile of v0, /device:TPU:0, one launch (start us, length us, event | category | flops | bytes accessed | tf_op | source)
XLA Modules:
  0.0 442.4 jit_solution(2750653464107480190)
XLA Ops:
  7.2 0.7 all-gather.2.cloned.1.call-update
  8.0 57.2 %all-gather.2.cloned.1.call-done = bf16[2048,1024]{1,0:T(8,128)(2,1)} async-done(((bf16[512,1024]{1,0:T(8,128)(2,1)}), bf16[2048,1024]{1,0:T(8,128)(2,1)}) %all-gather.2.cloned.1.call-update) | async-done | bytes 4194320 | tf_op jit(solution)/shard_map/all_gather | solution.py:31
  65.2 4.8 %fusion.36 = f32[2048,256]{1,0:T(8,128)} fusion(bf16[2048,1024]{1,0:T(8,128)(2,1)} %all-gather.2.cloned.1.call-done, bf16[1024,256]{1,0:T(8,128)(2,1)S(1)} %copy-done), kind=kOutput, calls=%fused_computation.78 | convolution fusion | flops 1073741824 | bytes 6815744 | tf_op jit(solution)/shard_map/dot_general | solution.py:33
  70.0 4.4 convolution_bitcast_fusion
  74.5 31.6 %reduce-scatter.8.cloned.1.call-done = f32[256,256]{1,0:T(8,128)} async-done(((f32[2048,256]{1,0:T(8,128)}), f32[256,256]{1,0:T(8,128)}) %reduce-scatter.8.cloned.1.call-update) | async-done | bytes 262160 | tf_op jit(solution)/shard_map/reduce_scatter | solution.py:32
  106.1 2.4 fusion.37
  108.8 30.9 %reduce-scatter.10.cloned.1.call-done = f32[256,4]{1,0:T(8,128)} async-done(((f32[2048,4]{1,0:T(8,128)}), f32[256,4]{1,0:T(8,128)}) %reduce-scatter.10.cloned.1.call-update) | async-done | bytes 4112
  139.7 1.0 copy.18
  140.7 54.8 %all-reduce.3.cloned.1.call-done = f32[256,256]{0,1:T(8,128)} async-done(((f32[256,256]{0,1:T(8,128)}), f32[256,256]{0,1:T(8,128)}) %all-reduce.3.cloned.1.call-update) | async-done | bytes 262160 | tf_op jit(solution)/shard_map/psum | solution.py:42
  195.5 1.1 copy.11
  196.6 1.0 fusion.11
  197.6 11.7 %cholesky.64 = f32[128,128]{1,0:T(8,128)S(1)} custom-call(f32[128,128]{1,0:T(8,128)S(1)} %cholesky.153), custom_call_target="Cholesky" | custom-call | tf_op jit(solution)/shard_map/jit(cholesky)/cholesky | solution.py:43
  209.4 9.8 %custom-call.23 = f32[1,128,128]{1,2,0:T(8,128)S(1)} custom-call(f32[1,128,128]{2,1,0:T(8,128)S(1)} %get-tuple-element.206), custom_call_target="InvertDiagBlocksLowerTriangular" | custom-call | tf_op jit(solution)/shard_map/jit(cholesky)/cholesky | solution.py:43
  219.7 11.7 %cholesky.131 = f32[128,128]{1,0:T(8,128)S(1)} custom-call(f32[128,128]{1,0:T(8,128)S(1)} %convolution_subtract_fusion.3), custom_call_target="Cholesky" | custom-call | tf_op jit(solution)/shard_map/jit(cholesky)/cholesky | solution.py:43
  231.4 0.7 compare_reduce_fusion.1
  233.5 4.2 while.27
  234.4 1.3 bitcast_dynamic-update-slice_fusion.4
  236.4 1.3 bitcast_dynamic-update-slice_fusion.4
  237.8 19.7 %custom-call.31 = f32[2,128,128]{1,2,0:T(8,128)S(1)} custom-call(f32[2,128,128]{2,1,0:T(8,128)S(1)} %get-tuple-element.168), custom_call_target="InvertDiagBlocksLowerTriangular" | custom-call | tf_op jit(solution)/shard_map/triangular_solve/custom-call.4 | solution.py:24
  257.4 133.4 %while.26 = (s32[]{:T(128)}, f32[4,256]{1,0:T(4,128)S(1)}, f32[4,256]{1,0:T(4,128)S(1)}, s32[]{:T(128)}, f32[256,256]{1,0:T(8,128)S(1)}, /*index=5*/f32[256,256]{1,0:T(8,128)S(1)}, s32[]{:T(128)}, s32[]{:T(128)}, s32[]{:T(128)}) while((s32[]{:T(128)}, f32[4,256]{1,0:T(4,128)S(1)}, f32[4,256]{1,0:T(4,128)S(1)}, s32[]{:T(128)}, ...), condition=%wide.region_9.12_spmd.clone, body=%wide.region_7.0_spmd.clone.sunk | while | flops 11149320 | bytes 1659231 | solution.py:60
  257.6 4.1 while.28
  258.3 1.3 bitcast_dynamic-update-slice_fusion.5
  260.3 1.3 bitcast_dynamic-update-slice_fusion.5
  261.6 19.7 %custom-call.37 = f32[2,128,128]{1,2,0:T(8,128)S(1)} custom-call(f32[2,128,128]{2,1,0:T(8,128)S(1)} %get-tuple-element.303), custom_call_target="InvertDiagBlocksLowerTriangular" | custom-call | tf_op jit(solution)/shard_map/while/body/eval_jaxpr/triangular_solve/custom-call.4 | solution.py:24
  281.5 13.7 %psum.45 = f32[256,4]{0,1:T(4,128)S(1)} all-reduce(f32[256,4]{0,1:T(4,128)S(1)} %fusion.99), channel_id=1, replica_groups=mesh['section'=4,'row'=8] {'row'}, use_global_device_ids=true, to_apply=%region_8.8 | all-reduce | flops 1024 | bytes 8192 | tf_op jit(solution)/shard_map/while/body/eval_jaxpr/psum | solution.py:47
  296.7 3.4 collective-permute-start
  300.1 1.3 collective-permute-done
  301.5 4.1 while.28
  302.2 1.3 bitcast_dynamic-update-slice_fusion.5
  304.2 1.3 bitcast_dynamic-update-slice_fusion.5
  305.6 19.7 %custom-call.37 = f32[2,128,128]{1,2,0:T(8,128)S(1)} custom-call(f32[2,128,128]{2,1,0:T(8,128)S(1)} %get-tuple-element.303), custom_call_target="InvertDiagBlocksLowerTriangular" | custom-call | tf_op jit(solution)/shard_map/while/body/eval_jaxpr/triangular_solve/custom-call.4 | solution.py:24
  325.5 13.6 %psum.45 = f32[256,4]{0,1:T(4,128)S(1)} all-reduce(f32[256,4]{0,1:T(4,128)S(1)} %fusion.99), channel_id=1, replica_groups=mesh['section'=4,'row'=8] {'row'}, use_global_device_ids=true, to_apply=%region_8.8 | all-reduce | flops 1024 | bytes 8192 | tf_op jit(solution)/shard_map/while/body/eval_jaxpr/psum | solution.py:47
  340.6 4.2 collective-permute-start
  344.8 1.3 collective-permute-done
  346.2 4.1 while.28
  346.2 0.7 fusion.106
  346.9 1.3 bitcast_dynamic-update-slice_fusion.5
  348.9 1.3 bitcast_dynamic-update-slice_fusion.5
  350.3 19.7 %custom-call.37 = f32[2,128,128]{1,2,0:T(8,128)S(1)} custom-call(f32[2,128,128]{2,1,0:T(8,128)S(1)} %get-tuple-element.303), custom_call_target="InvertDiagBlocksLowerTriangular" | custom-call | tf_op jit(solution)/shard_map/while/body/eval_jaxpr/triangular_solve/custom-call.4 | solution.py:24
  370.2 13.6 %psum.45 = f32[256,4]{0,1:T(4,128)S(1)} all-reduce(f32[256,4]{0,1:T(4,128)S(1)} %fusion.99), channel_id=1, replica_groups=mesh['section'=4,'row'=8] {'row'}, use_global_device_ids=true, to_apply=%region_8.8 | all-reduce | flops 1024 | bytes 8192 | tf_op jit(solution)/shard_map/while/body/eval_jaxpr/psum | solution.py:47
  385.2 4.3 collective-permute-start
  389.6 1.3 collective-permute-done
  391.1 13.6 %psum.40 = f32[256,4]{0,1:T(4,128)S(1)} all-reduce(f32[256,4]{0,1:T(4,128)S(1)} %fusion.38), channel_id=1, replica_groups=mesh['section'=4,'row'=8] {'row'}, use_global_device_ids=true, to_apply=%region_10.13 | all-reduce | flops 1024 | bytes 8192 | tf_op jit(solution)/shard_map/psum | solution.py:47
  405.9 1.0 convolution_bitcast_fusion.1
  407.2 11.0 %psum.41 = f32[4,256]{1,0:T(4,128)S(1)} all-reduce(f32[4,256]{1,0:T(4,128)S(1)} %fusion.10), channel_id=1, replica_groups=mesh['section'=4,'row'=8] {'section'}, use_global_device_ids=true, to_apply=%region_11.14 | all-reduce | flops 1024 | bytes 8192 | tf_op jit(solution)/shard_map/psum | solution.py:15
  418.3 13.6 %psum.42 = f32[4,4]{0,1:T(4,128)S(1)} all-reduce(f32[4,4]{0,1:T(4,128)S(1)} %fusion.39), channel_id=1, replica_groups=mesh['section'=4,'row'=8] {'row'}, use_global_device_ids=true, to_apply=%region_12.15 | all-reduce | flops 16 | bytes 128 | tf_op jit(solution)/shard_map/psum | solution.py:73
  434.1 1.0 copy.20
  435.0 0.8 fusion.22
  (100 shorter events, 15.1 us)
Async XLA Ops:
  7.2 58.0 %copy-start = (bf16[1024,256]{1,0:T(8,128)(2,1)S(1)}, bf16[1024,256]{1,0:T(8,128)(2,1)}, u32[]{:S(2)}) copy-start(bf16[1024,256]{1,0:T(8,128)(2,1)} %param.10) | copy-start | bytes 1572868
  7.2 58.0 %all-gather.2.cloned.1.call-start = ((), (), s32[]{:S(2)}) async-start(), calls=%async_computation.3 | async-start | bytes 5242880 | tf_op jit(solution)/shard_map/all_gather | solution.py:31
  7.9 62.1 %copy-start.3 = (bf16[4,1024]{1,0:T(4,128)(2,1)S(1)}, bf16[4,1024]{1,0:T(4,128)(2,1)}, u32[]{:S(2)}) copy-start(bf16[4,1024]{1,0:T(4,128)(2,1)} %param.11) | copy-start | bytes 24580
  7.9 98.2 %reduce-scatter.8.cloned.1.call-start = ((), (), s32[]{:S(2)}) async-start(), calls=%async_computation.4 | async-start | bytes 2359296 | tf_op jit(solution)/shard_map/reduce_scatter | solution.py:32
  70.0 69.7 %reduce-scatter.10.cloned.1.call-start = ((), (), s32[]{:S(2)}) async-start(), calls=%async_computation.6 | async-start | bytes 1179648
  74.5 121.0 %all-reduce.3.cloned.1.call-start = ((), (), s32[]{:S(2)}) async-start(), calls=%async_computation.5 | async-start | bytes 524288 | tf_op jit(solution)/shard_map/psum | solution.py:42
  106.1 151.3 %copy-start.1 = (f32[256,256]{1,0:T(8,128)S(1)}, f32[256,256]{1,0:T(8,128)}, u32[]{:S(2)}) copy-start(f32[256,256]{1,0:T(8,128)} %reduce-scatter.8.cloned.1.call-done) | copy-start | bytes 786436
  108.5 325.5 %reduce-scatter.12.cloned.1.call-start = ((), (), s32[]{:S(2)}) async-start(), calls=%async_computation.7 | async-start | bytes 655360
  296.7 4.7 %collective-permute-start = (f32[4,256]{1,0:T(4,128)S(1)}, f32[4,256]{1,0:T(4,128)S(1)}, u32[]{:S(2)}, u32[]{:S(2)}) collective-permute-start(f32[4,256]{1,0:T(4,128)S(1)} %fusion.104), channel_id=1, source_target_pairs={{0,8},{8,16},{16,24},{1,9},{9,17},{17,25},{2,10},{10,18},{18,26},{... | collective-permute-start | bytes 12296 | tf_op jit(solution)/shard_map/while/body/eval_jaxpr/ppermute | solution.py:10
  340.6 5.6 %collective-permute-start = (f32[4,256]{1,0:T(4,128)S(1)}, f32[4,256]{1,0:T(4,128)S(1)}, u32[]{:S(2)}, u32[]{:S(2)}) collective-permute-start(f32[4,256]{1,0:T(4,128)S(1)} %fusion.104), channel_id=1, source_target_pairs={{0,8},{8,16},{16,24},{1,9},{9,17},{17,25},{2,10},{10,18},{18,26},{... | collective-permute-start | bytes 12296 | tf_op jit(solution)/shard_map/while/body/eval_jaxpr/ppermute | solution.py:10
  385.2 5.6 %collective-permute-start = (f32[4,256]{1,0:T(4,128)S(1)}, f32[4,256]{1,0:T(4,128)S(1)}, u32[]{:S(2)}, u32[]{:S(2)}) collective-permute-start(f32[4,256]{1,0:T(4,128)S(1)} %fusion.104), channel_id=1, source_target_pairs={{0,8},{8,16},{16,24},{1,9},{9,17},{17,25},{2,10},{10,18},{18,26},{... | collective-permute-start | bytes 12296 | tf_op jit(solution)/shard_map/while/body/eval_jaxpr/ppermute | solution.py:10
  405.9 30.0 %copy-start.2 = (f32[4,256]{1,0:T(4,128)}, f32[4,256]{1,0:T(4,128)S(1)}, u32[]{:S(2)}) copy-start(f32[4,256]{1,0:T(4,128)S(1)} %bitcast_select_fusion.1) | copy-start | bytes 12292
Sparse Core Ops, SparseCore 0:
  9.8 55.2 all-gather.1
  70.1 35.9 reduce-scatter.7
  108.4 31.2 reduce-scatter.9
  141.9 53.5 all-reduce.2
  407.1 25.7 reduce-scatter.11
where the time goes:
time: 443 us; the launch traced here: 442 us
  waiting for transfers between devices  179 us (40%)
  other arithmetic  116 us (26%)
  blocking collectives  79.1 us (18%)
  matrix products  20.6 us (5%)
  local copies, waits for them, and re-layouts  19.6 us (4%)
  between operations  15.2 us (3%)
  starting transfers between devices  12.4 us (3%)
    another operation x16, other arithmetic, factor_solve(): lax.linalg.triangular_solve(factor, half, left_side=True, lower=True, tra...  78.8 us
    all_gather x1, waiting for transfers between devices, body(): whole = lax.all_gather(omega, 'section', axis=0, tiled=True)  57.2 us
    psum x1, waiting for transfers between devices, body(): gram = lax.psum(jnp.dot(sketch.T, sketch, precision=hi), 'row')  54.8 us
    psum x4, blocking collectives, project(): inner = lax.psum(inner, 'row')  54.5 us
    another operation x6, other arithmetic, body(): factor = jnp.linalg.cholesky(gram)  34 us
    unnamed x7, waiting for transfers between devices  31.7 us
    reduce_scatter x1, waiting for transfers between devices, body(): lax.psum_scatter(jnp.dot(whole, basis, preferred_element_type=jnp.float32...  31.6 us
    another operation x28, local copies, waits for them, and re-layouts, factor_solve(): lax.linalg.triangular_solve(factor, half, left_side=True, lower=True, tra...  16.4 us
  transfers between devices with their start and end apart: 8, of which 7 were waited for; matrix products, arithmetic and copies ran while one was open for 2% of the time, Pallas kernels for 0%

commit v1 on v0

--- a/solution.py
+++ b/solution.py
@@ -1,7 +1,22 @@
+import functools
 import jax
 import jax.numpy as jnp
 from jax import lax
 from jax.sharding import PartitionSpec as P
+
+
+def _enter_lots_all(inp, device_axis):
+    dev_count = lax.axis_size(device_axis)
+    p_next = inp
+    for q in [
+        [(nth, nth ^ t) for nth in range(dev_count)] for t in (1, 2, 4, 8, 16) if t < dev_count
+    ]:
+        u1 = lax.ppermute(p_next, device_axis, q)
+        p_next = p_next + u1
+    return p_next
+
+
+step_on_chains_now = functools.partial(_enter_lots_all, device_axis="row")
 
 
 def from_behind(value, axis, steps):
@@ -44,7 +59,7 @@
 
     def project(current):
         inner = jnp.dot(current, sketch, precision=hi)
-        inner = lax.psum(inner, "row")
+        inner = step_on_chains_now(inner)
         coef = factor_solve(factor, inner.T).T
         return (coef, current - jnp.dot(coef, sketch.T, precision=hi))
 

time: 443 us -> 412 us (0.930)
  blocking collectives: 79.1 us -> 24.6 us
  waiting for transfers between devices: 179 us -> 196 us
  starting transfers between devices: 12.4 us -> 20.3 us
    psum x4 -> x0, blocking collectives: 54.5 us -> none  [project(): inner = lax.psum(inner, 'row')]
    ppermute x0 -> x12, waiting for transfers between devices: none -> 17 us  [_enter_lots_all(): u1 = lax.ppermute(p_next, device_axis, q)]
    ppermute x0 -> x12, starting transfers between devices: none -> 7.95 us  [_enter_lots_all(): u1 = lax.ppermute(p_next, device_axis, q)]
  transfers between devices with their start and end apart: 8 -> 20, of which waited for: 7 -> 15; matrix products, arithmetic and copies ran while one was open for 2% -> 25% of each run, Pallas kernels for 0% -> 0%
where the time goes in v1:
time: 412 us
  waiting for transfers between devices  196 us (48%)
  other arithmetic  116 us (28%)
  blocking collectives  24.6 us (6%)
  matrix products  20.5 us (5%)
  starting transfers between devices  20.3 us (5%)
  local copies, waits for them, and re-layouts  18.5 us (4%)
  between operations  15.2 us (4%)
    another operation x16, other arithmetic, factor_solve(): lax.linalg.triangular_solve(factor, half, left_side=True, lower=True, tra...  78.9 us
    all_gather x1, waiting for transfers between devices, body(): whole = lax.all_gather(omega, 'section', axis=0, tiled=True)  57.2 us
    psum x1, waiting for transfers between devices, body(): gram = lax.psum(jnp.dot(sketch.T, sketch, precision=hi), 'row')  54.8 us
    another operation x6, other arithmetic, body(): factor = jnp.linalg.cholesky(gram)  34 us
    unnamed x7, waiting for transfers between devices  31.7 us
    reduce_scatter x1, waiting for transfers between devices, body(): lax.psum_scatter(jnp.dot(whole, basis, preferred_element_type=jnp.float32...  31.6 us
    ppermute x12, waiting for transfers between devices, _enter_lots_all(): u1 = lax.ppermute(p_next, device_axis, q)  17 us
    another operation x28, local copies, waits for them, and re-layouts, factor_solve(): lax.linalg.triangular_solve(factor, half, left_side=True, lower=True, tra...  15.3 us
  transfers between devices with their start and end apart: 20, of which 15 were waited for; matrix products, arithmetic and copies ran while one was open for 25% of the time, Pallas kernels for 0%

profile of v1, /device:TPU:0, one launch (start us, length us, event | category | flops | bytes accessed | tf_op | source)
XLA Modules:
  0.0 411.8 jit_solution(8188052149994774571)
XLA Ops:
  8.0 57.2 %all-gather.2.cloned.1.call-done = bf16[2048,1024]{1,0:T(8,128)(2,1)} async-done(((bf16[512,1024]{1,0:T(8,128)(2,1)}), bf16[2048,1024]{1,0:T(8,128)(2,1)}) %all-gather.2.cloned.1.call-update) | async-done | bytes 4194320 | tf_op jit(solution)/shard_map/all_gather | solution.py:46
  65.2 4.8 %fusion.38 = f32[2048,256]{1,0:T(8,128)} fusion(bf16[2048,1024]{1,0:T(8,128)(2,1)} %all-gather.2.cloned.1.call-done, bf16[1024,256]{1,0:T(8,128)(2,1)S(1)} %copy-done), kind=kOutput, calls=%fused_computation.82 | convolution fusion | flops 1073741824 | bytes 6815744 | tf_op jit(solution)/shard_map/dot_general | solution.py:48
  70.0 4.4 %convolution_bitcast_fusion = f32[2048,4]{1,0:T(8,128)} fusion(bf16[4,1024]{1,0:T(4,128)(2,1)S(1)} %copy-done.3, bf16[2048,1024]{1,0:T(8,128)(2,1)} %all-gather.2.cloned.1.call-done), kind=kOutput, calls=%fused_computation.25 | convolution fusion | flops 16777216 | bytes 4235264
  74.5 31.6 %reduce-scatter.8.cloned.1.call-done = f32[256,256]{1,0:T(8,128)} async-done(((f32[2048,256]{1,0:T(8,128)}), f32[256,256]{1,0:T(8,128)}) %reduce-scatter.8.cloned.1.call-update) | async-done | bytes 262160 | tf_op jit(solution)/shard_map/reduce_scatter | solution.py:47
  106.1 2.4 fusion.39
  108.8 30.9 %reduce-scatter.10.cloned.1.call-done = f32[256,4]{1,0:T(8,128)} async-done(((f32[2048,4]{1,0:T(8,128)}), f32[256,4]{1,0:T(8,128)}) %reduce-scatter.10.cloned.1.call-update) | async-done | bytes 4112
  140.7 54.8 %all-reduce.3.cloned.1.call-done = f32[256,256]{0,1:T(8,128)} async-done(((f32[256,256]{0,1:T(8,128)}), f32[256,256]{0,1:T(8,128)}) %all-reduce.3.cloned.1.call-update) | async-done | bytes 262160 | tf_op jit(solution)/shard_map/psum | solution.py:57
  195.5 1.1 copy.11
  197.6 11.7 %cholesky.64 = f32[128,128]{1,0:T(8,128)S(1)} custom-call(f32[128,128]{1,0:T(8,128)S(1)} %cholesky.153), custom_call_target="Cholesky" | custom-call | tf_op jit(solution)/shard_map/jit(cholesky)/cholesky | solution.py:58
  209.4 9.8 %custom-call.23 = f32[1,128,128]{1,2,0:T(8,128)S(1)} custom-call(f32[1,128,128]{2,1,0:T(8,128)S(1)} %get-tuple-element.206), custom_call_target="InvertDiagBlocksLowerTriangular" | custom-call | tf_op jit(solution)/shard_map/jit(cholesky)/cholesky | solution.py:58
  219.7 11.7 %cholesky.131 = f32[128,128]{1,0:T(8,128)S(1)} custom-call(f32[128,128]{1,0:T(8,128)S(1)} %convolution_subtract_fusion.2), custom_call_target="Cholesky" | custom-call | tf_op jit(solution)/shard_map/jit(cholesky)/cholesky | solution.py:58
  233.3 110.6 %while.26 = (s32[]{:T(128)}, f32[4,256]{1,0:T(4,128)S(1)}, f32[4,256]{1,0:T(4,128)S(1)}, s32[]{:T(128)}, f32[256,256]{1,0:T(8,128)S(1)}, /*index=5*/f32[256,256]{1,0:T(8,128)S(1)}, s32[]{:T(128)}, s32[]{:T(128)}, s32[]{:T(128)}) while((s32[]{:T(128)}, f32[4,256]{1,0:T(4,128)S(1)}, f32[4,256]{1,0:T(4,128)S(1)}, s32[]{:T(128)}, ...), condition=%wide.region_8.11_spmd.clone, body=%wide.region_7.10_spmd.clone.sunk | while | flops 11151368 | bytes 1737183 | solution.py:75
  233.8 1.1 collective-permute-done
  235.5 3.1 collective-permute-done.1
  238.6 1.5 collective-permute-start.2
  240.1 3.8 while.28
  240.7 1.3 bitcast_dynamic-update-slice_fusion.5
  242.6 1.3 bitcast_dynamic-update-slice_fusion.5
  243.9 19.7 %custom-call.37 = f32[2,128,128]{1,2,0:T(8,128)S(1)} custom-call(f32[2,128,128]{2,1,0:T(8,128)S(1)} %get-tuple-element.303), custom_call_target="InvertDiagBlocksLowerTriangular" | custom-call | tf_op jit(solution)/shard_map/while/body/eval_jaxpr/triangular_solve/custom-call.4 | solution.py:39
  265.1 3.4 collective-permute-start.3
  268.5 1.3 collective-permute-done.3
  270.1 1.1 collective-permute-done
  271.7 3.1 collective-permute-done.1
  274.8 1.5 collective-permute-start.2
  276.3 3.8 while.28
  276.9 1.3 bitcast_dynamic-update-slice_fusion.5
  278.8 1.3 bitcast_dynamic-update-slice_fusion.5
  280.1 19.7 %custom-call.37 = f32[2,128,128]{1,2,0:T(8,128)S(1)} custom-call(f32[2,128,128]{2,1,0:T(8,128)S(1)} %get-tuple-element.303), custom_call_target="InvertDiagBlocksLowerTriangular" | custom-call | tf_op jit(solution)/shard_map/while/body/eval_jaxpr/triangular_solve/custom-call.4 | solution.py:39
  301.3 4.2 %collective-permute-start.3 = (f32[4,256]{1,0:T(4,128)S(1)}, f32[4,256]{1,0:T(4,128)S(1)}, u32[]{:S(2)}, u32[]{:S(2)}) collective-permute-start(f32[4,256]{1,0:T(4,128)S(1)} %fusion.104), channel_id=1, source_target_pairs={{0,8},{8,16},{16,24},{1,9},{9,17},{17,25},{2,10},{10,18},{18,26},{... | collective-permute-start | bytes 12296 | tf_op jit(solution)/shard_map/while/body/eval_jaxpr/ppermute | solution.py:25
  305.6 1.3 collective-permute-done.3
  307.1 1.1 collective-permute-done
  308.8 3.1 collective-permute-done.1
  311.9 1.5 collective-permute-start.2
  313.4 3.8 while.28
  314.0 1.3 bitcast_dynamic-update-slice_fusion.5
  315.9 1.3 bitcast_dynamic-update-slice_fusion.5
  317.2 19.7 %custom-call.37 = f32[2,128,128]{1,2,0:T(8,128)S(1)} custom-call(f32[2,128,128]{2,1,0:T(8,128)S(1)} %get-tuple-element.303), custom_call_target="InvertDiagBlocksLowerTriangular" | custom-call | tf_op jit(solution)/shard_map/while/body/eval_jaxpr/triangular_solve/custom-call.4 | solution.py:39
  338.3 4.3 %collective-permute-start.3 = (f32[4,256]{1,0:T(4,128)S(1)}, f32[4,256]{1,0:T(4,128)S(1)}, u32[]{:S(2)}, u32[]{:S(2)}) collective-permute-start(f32[4,256]{1,0:T(4,128)S(1)} %fusion.104), channel_id=1, source_target_pairs={{0,8},{8,16},{16,24},{1,9},{9,17},{17,25},{2,10},{10,18},{18,26},{... | collective-permute-start | bytes 12296 | tf_op jit(solution)/shard_map/while/body/eval_jaxpr/ppermute | solution.py:25
  342.7 1.3 collective-permute-done.3
  344.2 1.2 collective-permute-done.4
  345.9 3.1 collective-permute-done.5
  349.0 1.5 collective-permute-start.6
  350.5 3.8 while.27
  351.1 1.3 bitcast_dynamic-update-slice_fusion.4
  353.0 1.3 bitcast_dynamic-update-slice_fusion.4
  354.3 19.7 %custom-call.31 = f32[2,128,128]{1,2,0:T(8,128)S(1)} custom-call(f32[2,128,128]{2,1,0:T(8,128)S(1)} %get-tuple-element.168), custom_call_target="InvertDiagBlocksLowerTriangular" | custom-call | tf_op jit(solution)/shard_map/triangular_solve/custom-call.4 | solution.py:39
  376.6 11.1 %psum.22 = f32[4,256]{1,0:T(4,128)S(1)} all-reduce(f32[4,256]{1,0:T(4,128)S(1)} %fusion.11), channel_id=1, replica_groups=mesh['section'=4,'row'=8] {'section'}, use_global_device_ids=true, to_apply=%region_9.12 | all-reduce | flops 1024 | bytes 8192 | tf_op jit(solution)/shard_map/psum | solution.py:30
  387.8 13.6 %psum.23 = f32[4,4]{0,1:T(4,128)S(1)} all-reduce(f32[4,4]{0,1:T(4,128)S(1)} %fusion.41), channel_id=1, replica_groups=mesh['section'=4,'row'=8] {'row'}, use_global_device_ids=true, to_apply=%region_10.13 | all-reduce | flops 16 | bytes 128 | tf_op jit(solution)/shard_map/psum | solution.py:88
  (132 shorter events, 23.3 us)
Async XLA Ops:
  7.2 58.0 %copy-start = (bf16[1024,256]{1,0:T(8,128)(2,1)S(1)}, bf16[1024,256]{1,0:T(8,128)(2,1)}, u32[]{:S(2)}) copy-start(bf16[1024,256]{1,0:T(8,128)(2,1)} %param.10) | copy-start | bytes 1572868
  7.2 58.0 %all-gather.2.cloned.1.call-start = ((), (), s32[]{:S(2)}) async-start(), calls=%async_computation.3 | async-start | bytes 5242880 | tf_op jit(solution)/shard_map/all_gather | solution.py:46
  7.9 62.1 %copy-start.3 = (bf16[4,1024]{1,0:T(4,128)(2,1)S(1)}, bf16[4,1024]{1,0:T(4,128)(2,1)}, u32[]{:S(2)}) copy-start(bf16[4,1024]{1,0:T(4,128)(2,1)} %param.11) | copy-start | bytes 24580
  7.9 98.2 %reduce-scatter.8.cloned.1.call-start = ((), (), s32[]{:S(2)}) async-start(), calls=%async_computation.4 | async-start | bytes 2359296 | tf_op jit(solution)/shard_map/reduce_scatter | solution.py:47
  70.0 69.7 %reduce-scatter.10.cloned.1.call-start = ((), (), s32[]{:S(2)}) async-start(), calls=%async_computation.6 | async-start | bytes 1179648
  74.5 121.1 %all-reduce.3.cloned.1.call-start = ((), (), s32[]{:S(2)}) async-start(), calls=%async_computation.5 | async-start | bytes 524288 | tf_op jit(solution)/shard_map/psum | solution.py:57
  106.1 127.2 %copy-start.1 = (f32[256,256]{1,0:T(8,128)S(1)}, f32[256,256]{1,0:T(8,128)}, u32[]{:S(2)}) copy-start(f32[256,256]{1,0:T(8,128)} %reduce-scatter.8.cloned.1.call-done) | copy-start | bytes 786436
  108.5 295.0 %reduce-scatter.12.cloned.1.call-start = ((), (), s32[]{:S(2)}) async-start(), calls=%async_computation.7 | async-start | bytes 655360
  233.8 1.2 collective-permute-start
  235.0 3.6 collective-permute-start.1
  238.6 25.0 %collective-permute-start.2 = (f32[4,256]{1,0:T(4,128)S(1)}, f32[4,256]{1,0:T(4,128)S(1)}, u32[]{:S(2)}, u32[]{:S(2)}) collective-permute-start(f32[4,256]{1,0:T(4,128)S(1)} %add.125), channel_id=1, source_target_pairs={{0,4},{1,5},{2,6},{3,7},{4,0},{5,1},{6,2},{7,3},{8,12},{9,13},{10,... | collective-permute-start | bytes 12296 | tf_op jit(solution)/shard_map/while/body/eval_jaxpr/ppermute | solution.py:14
  265.1 4.7 %collective-permute-start.3 = (f32[4,256]{1,0:T(4,128)S(1)}, f32[4,256]{1,0:T(4,128)S(1)}, u32[]{:S(2)}, u32[]{:S(2)}) collective-permute-start(f32[4,256]{1,0:T(4,128)S(1)} %fusion.104), channel_id=1, source_target_pairs={{0,8},{8,16},{16,24},{1,9},{9,17},{17,25},{2,10},{10,18},{18,26},{... | collective-permute-start | bytes 12296 | tf_op jit(solution)/shard_map/while/body/eval_jaxpr/ppermute | solution.py:25
  270.0 1.2 collective-permute-start
  271.2 3.6 collective-permute-start.1
  274.8 25.0 %collective-permute-start.2 = (f32[4,256]{1,0:T(4,128)S(1)}, f32[4,256]{1,0:T(4,128)S(1)}, u32[]{:S(2)}, u32[]{:S(2)}) collective-permute-start(f32[4,256]{1,0:T(4,128)S(1)} %add.125), channel_id=1, source_target_pairs={{0,4},{1,5},{2,6},{3,7},{4,0},{5,1},{6,2},{7,3},{8,12},{9,13},{10,... | collective-permute-start | bytes 12296 | tf_op jit(solution)/shard_map/while/body/eval_jaxpr/ppermute | solution.py:14
  301.3 5.6 %collective-permute-start.3 = (f32[4,256]{1,0:T(4,128)S(1)}, f32[4,256]{1,0:T(4,128)S(1)}, u32[]{:S(2)}, u32[]{:S(2)}) collective-permute-start(f32[4,256]{1,0:T(4,128)S(1)} %fusion.104), channel_id=1, source_target_pairs={{0,8},{8,16},{16,24},{1,9},{9,17},{17,25},{2,10},{10,18},{18,26},{... | collective-permute-start | bytes 12296 | tf_op jit(solution)/shard_map/while/body/eval_jaxpr/ppermute | solution.py:25
  307.0 1.2 collective-permute-start
  308.2 3.6 collective-permute-start.1
  311.9 25.0 %collective-permute-start.2 = (f32[4,256]{1,0:T(4,128)S(1)}, f32[4,256]{1,0:T(4,128)S(1)}, u32[]{:S(2)}, u32[]{:S(2)}) collective-permute-start(f32[4,256]{1,0:T(4,128)S(1)} %add.125), channel_id=1, source_target_pairs={{0,4},{1,5},{2,6},{3,7},{4,0},{5,1},{6,2},{7,3},{8,12},{9,13},{10,... | collective-permute-start | bytes 12296 | tf_op jit(solution)/shard_map/while/body/eval_jaxpr/ppermute | solution.py:14
  338.3 5.6 %collective-permute-start.3 = (f32[4,256]{1,0:T(4,128)S(1)}, f32[4,256]{1,0:T(4,128)S(1)}, u32[]{:S(2)}, u32[]{:S(2)}) collective-permute-start(f32[4,256]{1,0:T(4,128)S(1)} %fusion.104), channel_id=1, source_target_pairs={{0,8},{8,16},{16,24},{1,9},{9,17},{17,25},{2,10},{10,18},{18,26},{... | collective-permute-start | bytes 12296 | tf_op jit(solution)/shard_map/while/body/eval_jaxpr/ppermute | solution.py:25
  344.2 1.2 collective-permute-start.4
  345.4 3.6 collective-permute-start.5
  349.0 25.0 %collective-permute-start.6 = (f32[4,256]{1,0:T(4,128)S(1)}, f32[4,256]{1,0:T(4,128)S(1)}, u32[]{:S(2)}, u32[]{:S(2)}) collective-permute-start(f32[4,256]{1,0:T(4,128)S(1)} %add.96), channel_id=1, source_target_pairs={{0,4},{1,5},{2,6},{3,7},{4,0},{5,1},{6,2},{7,3},{8,12},{9,13},{10,... | collective-permute-start | bytes 12296 | tf_op jit(solution)/shard_map/ppermute | solution.py:14
  375.2 30.1 %copy-start.2 = (f32[4,256]{1,0:T(4,128)}, f32[4,256]{1,0:T(4,128)S(1)}, u32[]{:S(2)}) copy-start(f32[4,256]{1,0:T(4,128)S(1)} %bitcast_select_fusion.1) | copy-start | bytes 12292
Sparse Core Ops, SparseCore 0:
  9.8 55.2 all-gather.1
  70.1 35.9 reduce-scatter.7
  108.4 31.2 reduce-scatter.9
  141.9 53.5 all-reduce.2
  376.4 26.6 reduce-scatter.11
